TPU v7x, 32 devices: a whole 2x2x4 slice. The times are simulated.
32 devices in a mesh: af: 16 (over z, y, x), sa: 2 (over core).
Axes of the slice: x: 2, y: 2, z: 4, core: 2. Of those that a mesh axis runs over, the one named last changes fastest.
Arguments:
- series: float32 [8, 262144], P('sa', 'af'), parts along dimension 0, may hold values from -48 to 48
- tapers: float32 [10, 262144], P(None, 'af'), may hold values from -16 to 16
- concentration: float32 [10], replicated, may hold values from 0.2 to 0.95
- qi_weights: float32 [4, 10, 10], replicated, may hold values from -0.625 to 0.625
Outputs:
- spectrum: float32 [8, 16, 16384], P('sa', 'af'), parts along dimension 0
- qi_terms: float32 [8, 4, 16, 16384], P('sa', None, 'af'), parts along dimension 0
There are 2 independent parts, one for each index of `sa`. A program takes and returns all parts, laid end to end along the dimension named above; an argument that names none is the same for every part. Nothing has to cross between parts.
All inputs are finite; a program needn't handle non-finite values.
Results may differ from a plain program's by a relative error of at most 0.0001.
Values sent between devices are 32-bit elements; how exact they have to be, the bound alone decides.
A program may use at most 128 MiB of HBM per device.

v0:
```python
import math
import jax
import jax.numpy as jnp
from jax import lax
from jax.sharding import PartitionSpec as P

ITERS = 3


def fourier_table(length):
    indices = jnp.arange(length, dtype=jnp.int32)
    product = indices[:, None] * indices[None, :] % length
    angles = product.astype(jnp.float32) * (2.0 * math.pi / length)
    return (jnp.cos(angles), jnp.sin(angles))


def spectral_mean(estimate, length_all):
    return lax.psum(jnp.sum(estimate, axis=1), "af") / length_all


def local(series, tapers, concentration, qi_weights):
    highest = lax.Precision.HIGHEST
    shards = lax.axis_size("af")
    device_rank = lax.axis_index("af")
    series_count, local_len = series.shape
    taper_count = tapers.shape[0]
    block_len = local_len // shards
    length_all = local_len * shards
    unit_scale = 1.0 / math.sqrt(length_all)
    scaled = series * unit_scale
    got_series, got_tapers = (
        lax.all_to_all(
            scaled.reshape(series_count, shards, block_len),
            "af",
            split_axis=1,
            concat_axis=1,
            tiled=True,
        ),
        lax.all_to_all(
            tapers.reshape(taper_count, shards, block_len),
            "af",
            split_axis=1,
            concat_axis=1,
            tiled=True,
        ),
    )
    tapered = got_tapers[None] * got_series[:, None]
    cos_dev, sin_dev = fourier_table(shards)
    first_re = jnp.einsum("skpb,pc->skcb", tapered, cos_dev, precision=highest)
    first_im = -jnp.einsum("skpb,pc->skcb", tapered, sin_dev, precision=highest)
    sample_pos = device_rank * block_len + jnp.arange(block_len, dtype=jnp.int32)
    sample_phase = jnp.arange(shards, dtype=jnp.int32)[:, None] * sample_pos[None, :] % length_all
    angles = sample_phase.astype(jnp.float32) * (2.0 * math.pi / length_all)
    twist_cos = jnp.cos(angles)
    twist_sin = jnp.sin(angles)
    turned_re = first_re * twist_cos + first_im * twist_sin
    turned_im = first_im * twist_cos - first_re * twist_sin
    recv_re, recv_im = (
        lax.all_to_all(turned_re, "af", split_axis=2, concat_axis=2, tiled=True),
        lax.all_to_all(turned_im, "af", split_axis=2, concat_axis=2, tiled=True),
    )
    second_re = jnp.einsum("skrb,rc->skcb", recv_re, cos_dev, precision=highest) + jnp.einsum(
        "skrb,rc->skcb", recv_im, sin_dev, precision=highest
    )
    second_im = jnp.einsum("skrb,rc->skcb", recv_im, cos_dev, precision=highest) - jnp.einsum(
        "skrb,rc->skcb", recv_re, sin_dev, precision=highest
    )
    inner_phase = (
        jnp.arange(shards, dtype=jnp.int32)[:, None]
        * jnp.arange(block_len, dtype=jnp.int32)[None, :]
        % local_len
    )
    inner_angles = inner_phase.astype(jnp.float32) * (2.0 * math.pi / local_len)
    inner_cos = jnp.cos(inner_angles)
    inner_sin = jnp.sin(inner_angles)
    bent_re = second_re * inner_cos + second_im * inner_sin
    bent_im = second_im * inner_cos - second_re * inner_sin
    cos_blk, sin_blk = fourier_table(block_len)
    spec_re = jnp.einsum("skcb,bd->skdc", bent_re, cos_blk, precision=highest) + jnp.einsum(
        "skcb,bd->skdc", bent_im, sin_blk, precision=highest
    )
    spec_im = jnp.einsum("skcb,bd->skdc", bent_im, cos_blk, precision=highest) - jnp.einsum(
        "skcb,bd->skdc", bent_re, sin_blk, precision=highest
    )
    spec_re = spec_re.reshape(series_count, taper_count, local_len)
    spec_im = spec_im.reshape(series_count, taper_count, local_len)
    powers = spec_re * spec_re + spec_im * spec_im
    qi_list = []
    for term_index in range(qi_weights.shape[0]):
        mixed_re = jnp.einsum("jk,skf->sjf", qi_weights[term_index], spec_re, precision=highest)
        mixed_im = jnp.einsum("jk,skf->sjf", qi_weights[term_index], spec_im, precision=highest)
        qi_list.append(jnp.sum(spec_re * mixed_re + spec_im * mixed_im, axis=1))
    qi_terms = jnp.stack(qi_list, axis=1)
    retained = concentration[None, :, None]
    estimate = 0.5 * (powers[:, 0] + powers[:, 1])
    for sweep_index in range(ITERS):
        variance = spectral_mean(estimate, length_all)
        weight = (
            retained
            / (retained * estimate[:, None, :] + (1.0 - retained) * variance[:, None, None]) ** 2
        )
        estimate = jnp.sum(weight * powers, axis=1) / jnp.sum(weight, axis=1)
    return (
        estimate.reshape(series_count, 1, local_len),
        qi_terms.reshape(series_count, qi_terms.shape[1], 1, local_len),
    )


def solution(mesh):
    placed = (P("sa", "af"), P(None, "af"), P(), P())
    return jax.shard_map(
        local,
        mesh=mesh,
        in_specs=placed,
        out_specs=(P("sa", "af", None), P("sa", None, "af", None)),
        check_vma=False,
    )
```

profile of v0, /device:TPU:0, one launch (start us, length us, event | category | flops | bytes accessed | tf_op | source)
XLA Modules:
  0.0 598.7 jit_solution(10614809215614160121)
XLA Ops:
  2.3 8.3 %all-to-all-start.1 = ((f32[4,16,1024]{2,0,1:T(4,128)}), f32[4,16,1024]{2,0,1:T(4,128)S(1)}, u32[]{:S(2)}, u32[]{:S(2)}) async-start(f32[4,16,1024]{2,0,1:T(4,128)} %bitcast.5), calls=%async_computation.1 | async-start | bytes 524288 | tf_op jit(solution)/shard_map/all_to_all | solution.py:32
  14.0 6.6 %all-to-all-done.1 = f32[4,16,1024]{2,0,1:T(4,128)S(1)} async-done(((f32[4,16,1024]{2,0,1:T(4,128)}), f32[4,16,1024]{2,0,1:T(4,128)S(1)}, u32[]{:S(2)}, u32[]{:S(2)}) %all-to-all-start.1) | async-done | bytes 262176 | tf_op jit(solution)/shard_map/all_to_all | solution.py:32
  20.6 3.7 all-to-all-start
  24.7 23.2 %all-to-all-done = f32[10,16,1024]{2,0,1:T(8,128)S(1)} async-done(((f32[10,16,1024]{2,0,1:T(8,128)}), f32[10,16,1024]{2,0,1:T(8,128)S(1)}, u32[]{:S(2)}, u32[]{:S(2)}) %all-to-all-start) | async-done | bytes 655392 | tf_op jit(solution)/shard_map/all_to_all | solution.py:39
  48.3 2.5 fusion.34
  50.8 4.5 add_bitcast_fusion.1
  55.3 3.2 copy.155
  58.5 5.9 all-to-all-start.3
  64.4 5.0 copy.153
  69.3 45.9 %all-to-all-done.3 = f32[4,10,16,1024]{3,0,1,2:T(4,128)S(1)} async-done(((f32[4,10,16,1024]{3,0,1,2:T(4,128)}), f32[4,10,16,1024]{3,0,1,2:T(4,128)S(1)}, u32[]{:S(2)}, u32[]{:S(2)}) %all-to-all-start.3) | async-done | bytes 2621472 | tf_op jit(solution)/shard_map/all_to_all | solution.py:60
  115.2 12.3 %all-to-all-start.2 = ((f32[4,10,16,1024]{3,0,1,2:T(4,128)}), f32[4,10,16,1024]{3,0,1,2:T(4,128)}, u32[]{:S(2)}, u32[]{:S(2)}) async-start(f32[4,10,16,1024]{3,0,1,2:T(4,128)} %copy.153), calls=%async_computation.2 | async-start | bytes 5242880 | tf_op jit(solution)/shard_map/all_to_all | solution.py:59
  127.8 5.0 fusion.45
  132.9 5.1 fusion.47
  138.0 40.8 %all-to-all-done.2 = f32[4,10,16,1024]{3,0,1,2:T(4,128)} async-done(((f32[4,10,16,1024]{3,0,1,2:T(4,128)}), f32[4,10,16,1024]{3,0,1,2:T(4,128)}, u32[]{:S(2)}, u32[]{:S(2)}) %all-to-all-start.2) | async-done | bytes 2621472 | tf_op jit(solution)/shard_map/all_to_all | solution.py:59
  178.8 6.1 %fusion.70 = f32[16,4,10,1024]{3,0,2,1:T(8,128)S(1)} fusion(f32[16,4,10,1024]{3,0,2,1:T(8,128)} %fusion.45, f32[4,10,16,1024]{3,0,1,2:T(4,128)} %all-to-all-done.2), kind=kOutput, calls=%fused_computation.81 | convolution fusion | flops 126488064 | bytes 7864320 | tf_op jit(solution)/shard_map/skrb,rc->skcb/dot_general | solution.py:65
  185.0 17.2 %fusion.67 = f32[16,4,10,1024]{3,0,2,1:T(8,128)S(1)} fusion(f32[16,4,10,1024]{3,0,2,1:T(8,128)S(1)} %copy-done.3, f32[4,10,16,1024]{3,0,1,2:T(4,128)} %all-to-all-done.2), kind=kOutput, calls=%fused_computation.80 | convolution fusion | flops 126488064 | bytes 7864320 | tf_op jit(solution)/shard_map/skrb,rc->skcb/dot_general | solution.py:62
  202.1 25.0 %fusion.23 = f32[1024,4,10,16]{0,3,2,1:T(8,128)S(1)} fusion(f32[16,4,10,1024]{3,0,2,1:T(8,128)S(1)} %fusion.70, f32[16,4,10,1024]{3,0,2,1:T(8,128)S(1)} %fusion.67, f32[16,1024]{1,0:T(8,128)S(1)} %get-tuple-element.26, f32[16,1024]{1,0:T(8,128)S(1)} %get-tuple-element.27), kind=kOutput, calls=%fused_computation.34 | convolution fusion | flops 8069709824 | bytes 7995392 | tf_op jit(solution)/shard_map/skcb,bd->skdc/dot_general | solution.py:82
  227.1 25.3 %fusion.25 = f32[1024,4,10,16]{0,3,2,1:T(8,128)} fusion(f32[16,4,10,1024]{3,0,2,1:T(8,128)S(1)} %fusion.67, f32[16,4,10,1024]{3,0,2,1:T(8,128)S(1)} %fusion.70, f32[16,1024]{1,0:T(8,128)S(1)} %get-tuple-element.26, f32[16,1024]{1,0:T(8,128)S(1)} %get-tuple-element.27), kind=kOutput, calls=%fused_computation.36 | convolution fusion | flops 8069709824 | bytes 7995392 | tf_op jit(solution)/shard_map/skcb,bd->skdc/dot_general | solution.py:79
  252.5 24.6 %subtract_bitcast_fusion = f32[4,10,1024,16]{2,3,1,0:T(8,128)S(1)} fusion(f32[1024,4,10,16]{0,3,2,1:T(8,128)S(1)} %fusion.23, f32[16,4,10,1024]{3,0,2,1:T(8,128)S(1)} %fusion.67, f32[16,4,10,1024]{3,0,2,1:T(8,128)S(1)} %fusion.70, f32[16,1024]{1,0:T(8,128)S(1)} %get-tuple-element.26, f32[16,1024]{1,0:T(8,128)S(1)} %get-tuple-element.27), kind=kOutput, calls=%fused_computation.64 | convolution fusion | flops 8070365184 | bytes 10616832 | tf_op jit(solution)/shard_map/skcb,bd->skdc/dot_general | solution.py:82
  277.1 10.1 %copy.160 = f32[4,10,1024,16]{3,2,0,1:T(8,128)} copy(f32[4,10,1024,16]{2,3,1,0:T(8,128)S(1)} %subtract_bitcast_fusion) | data formatting | bytes 5242880 | tf_op jit(solution)/shard_map/sub | solution.py:82
  287.2 16.1 %reshape.261 = f32[4,10,16384]{2,0,1:T(4,128)} reshape(f32[4,10,1024,16]{3,2,0,1:T(8,128)} %copy.160) | data formatting | bytes 5242880 | tf_op jit(solution)/shard_map/reshape | solution.py:86
  303.3 27.8 %add_bitcast_fusion = f32[4,10,1024,16]{2,3,1,0:T(8,128)S(1)} fusion(f32[1024,4,10,16]{0,3,2,1:T(8,128)} %fusion.25, f32[16,4,10,1024]{3,0,2,1:T(8,128)} %copy-done.4, f32[16,4,10,1024]{3,0,2,1:T(8,128)} %copy-done.5, f32[16,1024]{1,0:T(8,128)S(1)} %get-tuple-element.26, f32[16,1024]{1,0:T(8,128)S(1)} %get-tuple-element.27), kind=kOutput, calls=%fused_computation.65 | convolution fusion | flops 8070365184 | bytes 10616832 | tf_op jit(solution)/shard_map/skcb,bd->skdc/dot_general | solution.py:79
  332.6 10.1 %copy.159 = f32[4,10,1024,16]{3,2,0,1:T(8,128)} copy(f32[4,10,1024,16]{2,3,1,0:T(8,128)S(1)} %add_bitcast_fusion) | data formatting | bytes 5242880 | tf_op jit(solution)/shard_map/add | solution.py:79
  342.7 14.9 %reshape.260 = f32[4,10,16384]{2,0,1:T(4,128)S(1)} reshape(f32[4,10,1024,16]{3,2,0,1:T(8,128)} %copy.159) | data formatting | bytes 5242880 | tf_op jit(solution)/shard_map/reshape | solution.py:85
  359.9 46.9 %psum.21 = f32[4]{0:T(128)S(1)} all-reduce(f32[4]{0:T(128)S(1)} %get-tuple-element.16), channel_id=1, replica_groups=mesh['af'=16,'sa'=2] {'af'}, use_global_device_ids=true, to_apply=%region_1.2 | all-reduce | flops 4 | bytes 32 | tf_op jit(solution)/shard_map/psum | solution.py:18
  406.8 2.0 mul.486
  408.9 2.2 copy.161
  411.2 3.5 multiply_reduce_fusion.2
  416.6 3.4 reduce_sum.133
  421.3 2.0 reduce_sum.132
  425.2 36.6 %psum.22 = f32[4]{0:T(128)S(1)} all-reduce(f32[4]{0:T(128)S(1)} %get-tuple-element.14), channel_id=1, replica_groups=mesh['af'=16,'sa'=2] {'af'}, use_global_device_ids=true, to_apply=%region_5.6 | all-reduce | flops 4 | bytes 32 | tf_op jit(solution)/shard_map/psum | solution.py:18
  461.9 2.2 copy.163
  464.2 3.5 multiply_reduce_fusion.1
  469.6 2.7 reduce_sum.138
  472.3 2.3 fusion.43
  474.6 2.0 reduce_sum.137
  477.5 38.8 %psum.23 = f32[4]{0:T(128)S(1)} all-reduce(f32[4]{0:T(128)S(1)} %get-tuple-element.12), channel_id=1, replica_groups=mesh['af'=16,'sa'=2] {'af'}, use_global_device_ids=true, to_apply=%region_9.10 | all-reduce | flops 4 | bytes 32 | tf_op jit(solution)/shard_map/psum | solution.py:18
  516.4 2.2 copy.166
  518.7 3.5 multiply_reduce_fusion
  524.1 2.7 reduce_sum.141
  529.2 7.3 %fusion.2 = f32[4,10,16384]{2,1,0:T(8,128)S(1)} fusion(f32[4,10,16384]{2,0,1:T(4,128)S(1)} %reshape.260, f32[1,10,10]{2,0,1:T(1,128)S(1)} %get-tuple-element.23), kind=kOutput, calls=%fused_computation.4 | convolution fusion | flops 79298560 | bytes 5243280 | tf_op jit(solution)/shard_map/jk,skf->sjf/dot_general | solution.py:90
  536.6 9.1 %fusion.82 = f32[4,16384]{1,0:T(4,128)S(1)} fusion(f32[4,10,16384]{2,1,0:T(8,128)S(1)} %fusion.2, f32[4,10,16384]{2,0,1:T(4,128)S(1)} %copy-done, f32[1,10,10]{2,0,1:T(1,128)S(1)} %get-tuple-element.23), kind=kOutput, calls=%fused_computation.85 | convolution fusion | flops 80543744 | bytes 5505424 | tf_op jit(solution)/shard_map/jk,skf->sjf/dot_general | solution.py:91
  545.9 7.3 %fusion.5 = f32[4,10,16384]{2,1,0:T(8,128)S(1)} fusion(f32[4,10,16384]{2,0,1:T(4,128)S(1)} %reshape.260, f32[1,10,10]{2,0,1:T(1,128)S(1)} %get-tuple-element.21), kind=kOutput, calls=%fused_computation.9 | convolution fusion | flops 79298560 | bytes 5243280 | tf_op jit(solution)/shard_map/jk,skf->sjf/dot_general | solution.py:90
  553.3 8.9 %fusion.79 = f32[4,16384]{1,0:T(4,128)S(1)} fusion(f32[4,10,16384]{2,1,0:T(8,128)S(1)} %fusion.5, f32[4,10,16384]{2,0,1:T(4,128)S(1)} %copy-done, f32[1,10,10]{2,0,1:T(1,128)S(1)} %get-tuple-element.21), kind=kOutput, calls=%fused_computation.84 | convolution fusion | flops 80543744 | bytes 5505424 | tf_op jit(solution)/shard_map/jk,skf->sjf/dot_general | solution.py:91
  562.4 7.3 %fusion.8 = f32[4,10,16384]{2,1,0:T(8,128)S(1)} fusion(f32[4,10,16384]{2,0,1:T(4,128)S(1)} %reshape.260, f32[1,10,10]{2,0,1:T(1,128)S(1)} %get-tuple-element.22), kind=kOutput, calls=%fused_computation.14 | convolution fusion | flops 79298560 | bytes 5243280 | tf_op jit(solution)/shard_map/jk,skf->sjf/dot_general | solution.py:90
  569.7 8.9 %fusion.76 = f32[4,16384]{1,0:T(4,128)S(1)} fusion(f32[4,10,16384]{2,1,0:T(8,128)S(1)} %fusion.8, f32[4,10,16384]{2,0,1:T(4,128)S(1)} %copy-done, f32[1,10,10]{2,0,1:T(1,128)S(1)} %get-tuple-element.22), kind=kOutput, calls=%fused_computation.83 | convolution fusion | flops 80543744 | bytes 5505424 | tf_op jit(solution)/shard_map/jk,skf->sjf/dot_general | solution.py:91
  578.8 7.3 %fusion.11 = f32[4,10,16384]{2,1,0:T(8,128)S(1)} fusion(f32[4,10,16384]{2,0,1:T(4,128)S(1)} %reshape.260, f32[1,10,10]{2,0,1:T(1,128)S(1)} %get-tuple-element.20), kind=kOutput, calls=%fused_computation.19 | convolution fusion | flops 79298560 | bytes 5243280 | tf_op jit(solution)/shard_map/jk,skf->sjf/dot_general | solution.py:90
  586.2 9.0 %fusion.73 = f32[4,16384]{1,0:T(4,128)S(1)} fusion(f32[4,10,16384]{2,1,0:T(8,128)S(1)} %fusion.11, f32[4,10,16384]{2,0,1:T(4,128)S(1)} %copy-done, f32[1,10,10]{2,0,1:T(1,128)S(1)} %get-tuple-element.20), kind=kOutput, calls=%fused_computation.82 | convolution fusion | flops 80543744 | bytes 5505424 | tf_op jit(solution)/shard_map/jk,skf->sjf/dot_general | solution.py:91
  (57 shorter events, 26.5 us)
Async XLA Ops:
  2.3 18.2 %all-to-all-start.1 = ((f32[4,16,1024]{2,0,1:T(4,128)}), f32[4,16,1024]{2,0,1:T(4,128)S(1)}, u32[]{:S(2)}, u32[]{:S(2)}) async-start(f32[4,16,1024]{2,0,1:T(4,128)} %bitcast.5), calls=%async_computation.1 | async-start | bytes 524288 | tf_op jit(solution)/shard_map/all_to_all | solution.py:32
  20.6 27.3 %all-to-all-start = ((f32[10,16,1024]{2,0,1:T(8,128)}), f32[10,16,1024]{2,0,1:T(8,128)S(1)}, u32[]{:S(2)}, u32[]{:S(2)}) async-start(f32[10,16,1024]{2,0,1:T(8,128)} %copy.150), calls=%async_computation | async-start | bytes 2097152 | tf_op jit(solution)/shard_map/all_to_all | solution.py:39
  58.5 56.7 %all-to-all-start.3 = ((f32[4,10,16,1024]{3,0,1,2:T(4,128)}), f32[4,10,16,1024]{3,0,1,2:T(4,128)S(1)}, u32[]{:S(2)}, u32[]{:S(2)}) async-start(f32[4,10,16,1024]{3,0,1,2:T(4,128)} %copy.155), calls=%async_computation.3 | async-start | bytes 5242880 | tf_op jit(solution)/shard_map/all_to_all | solution.py:60
  69.3 58.5 %copy-start.8 = (f32[10]{0:T(128)S(1)}, f32[10]{0:T(128)}, u32[]{:S(2)}) copy-start(f32[10]{0:T(128)} %param.6) | copy-start | bytes 124
  69.3 58.5 %copy-start.7 = (f32[4,10,10]{2,0,1:T(4,128)S(1)}, f32[4,10,10]{2,0,1:T(4,128)}, u32[]{:S(2)}) copy-start(f32[4,10,10]{2,0,1:T(4,128)} %param.7) | copy-start | bytes 4804
  115.2 63.6 %all-to-all-start.2 = ((f32[4,10,16,1024]{3,0,1,2:T(4,128)}), f32[4,10,16,1024]{3,0,1,2:T(4,128)}, u32[]{:S(2)}, u32[]{:S(2)}) async-start(f32[4,10,16,1024]{3,0,1,2:T(4,128)} %copy.153), calls=%async_computation.2 | async-start | bytes 5242880 | tf_op jit(solution)/shard_map/all_to_all | solution.py:59
  138.0 47.0 %copy-start.3 = (f32[16,4,10,1024]{3,0,2,1:T(8,128)S(1)}, f32[16,4,10,1024]{3,0,2,1:T(8,128)}, u32[]{:S(2)}) copy-start(f32[16,4,10,1024]{3,0,2,1:T(8,128)} %fusion.47) | copy-start | bytes 7864324
  184.9 67.5 %copy-start.4 = (f32[16,4,10,1024]{3,0,2,1:T(8,128)}, f32[16,4,10,1024]{3,0,2,1:T(8,128)S(1)}, u32[]{:S(2)}) copy-start(f32[16,4,10,1024]{3,0,2,1:T(8,128)S(1)} %fusion.70) | copy-start | bytes 7864324
  202.1 50.3 %copy-start.5 = (f32[16,4,10,1024]{3,0,2,1:T(8,128)}, f32[16,4,10,1024]{3,0,2,1:T(8,128)S(1)}, u32[]{:S(2)}) copy-start(f32[16,4,10,1024]{3,0,2,1:T(8,128)S(1)} %fusion.67) | copy-start | bytes 7864324
  277.1 10.2 %copy-start.1 = (f32[4,10,1024,16]{2,3,1,0:T(8,128)}, f32[4,10,1024,16]{2,3,1,0:T(8,128)S(1)}, u32[]{:S(2)}) copy-start(f32[4,10,1024,16]{2,3,1,0:T(8,128)S(1)} %subtract_bitcast_fusion) | copy-start | bytes 7864324
  331.1 1.5 copy-start.2
  522.1 4.7 copy-start.6
  529.2 7.3 %copy-start = (f32[4,10,16384]{2,0,1:T(4,128)S(1)}, f32[4,10,16384]{2,0,1:T(4,128)}, u32[]{:S(2)}) copy-start(f32[4,10,16384]{2,0,1:T(4,128)} %reshape.261) | copy-start | bytes 7864324
where the time goes:
time: 608 us; the launch traced here: 599 us
  matrix products  208 us (34%)
  blocking collectives  122 us (20%)
  waiting for transfers between devices  116 us (19%)
  local copies, waits for them, and re-layouts  95.8 us (16%)
  starting transfers between devices  30.2 us (5%)
  other arithmetic  24.1 us (4%)
    psum x3, blocking collectives, spectral_mean(): return lax.psum(jnp.sum(estimate, axis=1), 'af') / length_all  122 us
    all_to_all x1, waiting for transfers between devices, local(): lax.all_to_all(turned_im, 'af', split_axis=2, concat_axis=2, tiled=True)  45.9 us
    all_to_all x1, waiting for transfers between devices, local(): lax.all_to_all(turned_re, 'af', split_axis=2, concat_axis=2, tiled=True)  40.8 us
    dot_general x4, matrix products, local(): jnp.einsum('jk,skf->sjf', qi_weights[term_index], spec_im, precision=high...  35.9 us
    dot_general x4, matrix products, local(): jnp.einsum('jk,skf->sjf', qi_weights[term_index], spec_re, precision=high...  29.4 us
    dot_general x1, matrix products, local(): jnp.einsum('skcb,bd->skdc', bent_re, cos_blk, precision=highest)  27.8 us
    dot_general x1, matrix products, local(): jnp.einsum('skcb,bd->skdc', bent_im, sin_blk, precision=highest)  25.3 us
    dot_general x1, matrix products, local(): jnp.einsum('skcb,bd->skdc', bent_re, sin_blk, precision=highest)  25 us
  transfers between devices with their start and end apart: 4, of which 4 were waited for; matrix products, arithmetic and copies ran while one was open for 3% of the time, Pallas kernels for 0%

commit v1 on v0

--- a/solution.py
+++ b/solution.py
@@ -15,7 +15,7 @@
 
 
 def spectral_mean(estimate, length_all):
-    return lax.psum(jnp.sum(estimate, axis=1), "af") / length_all
+    return jnp.sum(lax.all_gather(jnp.sum(estimate, axis=1), "af"), axis=0) / length_all
 
 
 def local(series, tapers, concentration, qi_weights):

time: 608 us -> 610 us (level)
    psum x3 -> x0, blocking collectives: 122 us -> none  [spectral_mean(): return lax.psum(jnp.sum(estimate, axis=1), 'af') / length_all]
    unnamed x0 -> x3, blocking collectives: none -> 122 us
where the time goes in v1:
time: 610 us; the launch traced here: 600 us
  matrix products  208 us (34%)
  blocking collectives  122 us (20%)
  waiting for transfers between devices  115 us (19%)
  local copies, waits for them, and re-layouts  97.4 us (16%)
  starting transfers between devices  30.2 us (5%)
  other arithmetic  24.1 us (4%)
    unnamed x3, blocking collectives  122 us
    all_to_all x1, waiting for transfers between devices, local(): lax.all_to_all(turned_im, 'af', split_axis=2, concat_axis=2, tiled=True)  45.9 us
    all_to_all x1, waiting for transfers between devices, local(): lax.all_to_all(turned_re, 'af', split_axis=2, concat_axis=2, tiled=True)  39.6 us
    dot_general x4, matrix products, local(): jnp.einsum('jk,skf->sjf', qi_weights[term_index], spec_im, precision=high...  35.9 us
    dot_general x4, matrix products, local(): jnp.einsum('jk,skf->sjf', qi_weights[term_index], spec_re, precision=high...  29.4 us
    dot_general x1, matrix products, local(): jnp.einsum('skcb,bd->skdc', bent_re, cos_blk, precision=highest)  27.8 us
    dot_general x1, matrix products, local(): jnp.einsum('skcb,bd->skdc', bent_im, sin_blk, precision=highest)  25.3 us
    dot_general x1, matrix products, local(): jnp.einsum('skcb,bd->skdc', bent_re, sin_blk, precision=highest)  25 us
  transfers between devices with their start and end apart: 4, of which 4 were waited for; matrix products, arithmetic and copies ran while one was open for 3% of the time, Pallas kernels for 0%

profile of v1, /device:TPU:0, one launch (start us, length us, event | category | flops | bytes accessed | tf_op | source)
XLA Modules:
  0.0 599.8 jit_solution(6258064998376456479)
XLA Ops:
  2.3 8.3 %all-to-all-start.1 = ((f32[4,16,1024]{2,0,1:T(4,128)}), f32[4,16,1024]{2,0,1:T(4,128)S(1)}, u32[]{:S(2)}, u32[]{:S(2)}) async-start(f32[4,16,1024]{2,0,1:T(4,128)} %bitcast.5), calls=%async_computation.1 | async-start | bytes 524288 | tf_op jit(solution)/shard_map/all_to_all | solution.py:32
  14.0 6.6 %all-to-all-done.1 = f32[4,16,1024]{2,0,1:T(4,128)S(1)} async-done(((f32[4,16,1024]{2,0,1:T(4,128)}), f32[4,16,1024]{2,0,1:T(4,128)S(1)}, u32[]{:S(2)}, u32[]{:S(2)}) %all-to-all-start.1) | async-done | bytes 262176 | tf_op jit(solution)/shard_map/all_to_all | solution.py:32
  20.6 3.7 all-to-all-start
  24.7 23.2 %all-to-all-done = f32[10,16,1024]{2,0,1:T(8,128)S(1)} async-done(((f32[10,16,1024]{2,0,1:T(8,128)}), f32[10,16,1024]{2,0,1:T(8,128)S(1)}, u32[]{:S(2)}, u32[]{:S(2)}) %all-to-all-start) | async-done | bytes 655392 | tf_op jit(solution)/shard_map/all_to_all | solution.py:39
  48.3 2.5 fusion.34
  50.8 4.5 add_bitcast_fusion.1
  55.3 3.2 copy.155
  58.5 5.9 all-to-all-start.3
  64.4 5.0 copy.153
  69.3 45.9 %all-to-all-done.3 = f32[4,10,16,1024]{3,0,1,2:T(4,128)S(1)} async-done(((f32[4,10,16,1024]{3,0,1,2:T(4,128)}), f32[4,10,16,1024]{3,0,1,2:T(4,128)S(1)}, u32[]{:S(2)}, u32[]{:S(2)}) %all-to-all-start.3) | async-done | bytes 2621472 | tf_op jit(solution)/shard_map/all_to_all | solution.py:60
  115.2 12.3 %all-to-all-start.2 = ((f32[4,10,16,1024]{3,0,1,2:T(4,128)}), f32[4,10,16,1024]{3,0,1,2:T(4,128)}, u32[]{:S(2)}, u32[]{:S(2)}) async-start(f32[4,10,16,1024]{3,0,1,2:T(4,128)} %copy.153), calls=%async_computation.2 | async-start | bytes 5242880 | tf_op jit(solution)/shard_map/all_to_all | solution.py:59
  129.1 5.0 fusion.45
  134.1 5.1 fusion.47
  139.2 39.6 %all-to-all-done.2 = f32[4,10,16,1024]{3,0,1,2:T(4,128)} async-done(((f32[4,10,16,1024]{3,0,1,2:T(4,128)}), f32[4,10,16,1024]{3,0,1,2:T(4,128)}, u32[]{:S(2)}, u32[]{:S(2)}) %all-to-all-start.2) | async-done | bytes 2621472 | tf_op jit(solution)/shard_map/all_to_all | solution.py:59
  178.8 6.1 %fusion.70 = f32[16,4,10,1024]{3,0,2,1:T(8,128)S(1)} fusion(f32[16,4,10,1024]{3,0,2,1:T(8,128)} %fusion.45, f32[4,10,16,1024]{3,0,1,2:T(4,128)} %all-to-all-done.2), kind=kOutput, calls=%fused_computation.81 | convolution fusion | flops 126488064 | bytes 7864320 | tf_op jit(solution)/shard_map/skrb,rc->skcb/dot_general | solution.py:65
  185.0 17.2 %fusion.67 = f32[16,4,10,1024]{3,0,2,1:T(8,128)S(1)} fusion(f32[16,4,10,1024]{3,0,2,1:T(8,128)S(1)} %copy-done.3, f32[4,10,16,1024]{3,0,1,2:T(4,128)} %all-to-all-done.2), kind=kOutput, calls=%fused_computation.80 | convolution fusion | flops 126488064 | bytes 7864320 | tf_op jit(solution)/shard_map/skrb,rc->skcb/dot_general | solution.py:62
  202.2 25.0 %fusion.23 = f32[1024,4,10,16]{0,3,2,1:T(8,128)S(1)} fusion(f32[16,4,10,1024]{3,0,2,1:T(8,128)S(1)} %fusion.70, f32[16,4,10,1024]{3,0,2,1:T(8,128)S(1)} %fusion.67, f32[16,1024]{1,0:T(8,128)S(1)} %get-tuple-element.26, f32[16,1024]{1,0:T(8,128)S(1)} %get-tuple-element.27), kind=kOutput, calls=%fused_computation.34 | convolution fusion | flops 8069709824 | bytes 7995392 | tf_op jit(solution)/shard_map/skcb,bd->skdc/dot_general | solution.py:82
  227.2 25.3 %fusion.25 = f32[1024,4,10,16]{0,3,2,1:T(8,128)} fusion(f32[16,4,10,1024]{3,0,2,1:T(8,128)S(1)} %fusion.67, f32[16,4,10,1024]{3,0,2,1:T(8,128)S(1)} %fusion.70, f32[16,1024]{1,0:T(8,128)S(1)} %get-tuple-element.26, f32[16,1024]{1,0:T(8,128)S(1)} %get-tuple-element.27), kind=kOutput, calls=%fused_computation.36 | convolution fusion | flops 8069709824 | bytes 7995392 | tf_op jit(solution)/shard_map/skcb,bd->skdc/dot_general | solution.py:79
  252.5 24.6 %subtract_bitcast_fusion = f32[4,10,1024,16]{2,3,1,0:T(8,128)S(1)} fusion(f32[1024,4,10,16]{0,3,2,1:T(8,128)S(1)} %fusion.23, f32[16,4,10,1024]{3,0,2,1:T(8,128)S(1)} %fusion.67, f32[16,4,10,1024]{3,0,2,1:T(8,128)S(1)} %fusion.70, f32[16,1024]{1,0:T(8,128)S(1)} %get-tuple-element.26, f32[16,1024]{1,0:T(8,128)S(1)} %get-tuple-element.27), kind=kOutput, calls=%fused_computation.64 | convolution fusion | flops 8070365184 | bytes 10616832 | tf_op jit(solution)/shard_map/skcb,bd->skdc/dot_general | solution.py:82
  277.1 10.1 %copy.160 = f32[4,10,1024,16]{3,2,0,1:T(8,128)} copy(f32[4,10,1024,16]{2,3,1,0:T(8,128)S(1)} %subtract_bitcast_fusion) | data formatting | bytes 5242880 | tf_op jit(solution)/shard_map/sub | solution.py:82
  287.3 16.1 %reshape.267 = f32[4,10,16384]{2,0,1:T(4,128)} reshape(f32[4,10,1024,16]{3,2,0,1:T(8,128)} %copy.160) | data formatting | bytes 5242880 | tf_op jit(solution)/shard_map/reshape | solution.py:86
  303.3 27.8 %add_bitcast_fusion = f32[4,10,1024,16]{2,3,1,0:T(8,128)S(1)} fusion(f32[1024,4,10,16]{0,3,2,1:T(8,128)} %fusion.25, f32[16,4,10,1024]{3,0,2,1:T(8,128)} %copy-done.4, f32[16,4,10,1024]{3,0,2,1:T(8,128)} %copy-done.5, f32[16,1024]{1,0:T(8,128)S(1)} %get-tuple-element.26, f32[16,1024]{1,0:T(8,128)S(1)} %get-tuple-element.27), kind=kOutput, calls=%fused_computation.65 | convolution fusion | flops 8070365184 | bytes 10616832 | tf_op jit(solution)/shard_map/skcb,bd->skdc/dot_general | solution.py:79
  332.6 10.1 %copy.159 = f32[4,10,1024,16]{3,2,0,1:T(8,128)} copy(f32[4,10,1024,16]{2,3,1,0:T(8,128)S(1)} %add_bitcast_fusion) | data formatting | bytes 5242880 | tf_op jit(solution)/shard_map/add | solution.py:79
  342.7 14.9 %reshape.266 = f32[4,10,16384]{2,0,1:T(4,128)S(1)} reshape(f32[4,10,1024,16]{3,2,0,1:T(8,128)} %copy.159) | data formatting | bytes 5242880 | tf_op jit(solution)/shard_map/reshape | solution.py:85
  360.2 46.9 %all-reduce = f32[64]{0:T(128)S(1)} all-reduce(f32[64]{0:T(128)S(1)} %dynamic-update-slice), channel_id=2, replica_groups=mesh['af'=16,'sa'=2] {'af'}, use_global_device_ids=true, to_apply=%add | all-reduce | flops 64 | bytes 512
  407.2 2.0 mul.486
  409.2 2.2 copy.161
  411.6 3.5 multiply_reduce_fusion.2
  417.0 3.4 reduce_sum.161
  421.7 2.0 reduce_sum.160
  425.8 36.5 %all-reduce.1 = f32[64]{0:T(128)S(1)} all-reduce(f32[64]{0:T(128)S(1)} %dynamic-update-slice.1), channel_id=3, replica_groups=mesh['af'=16,'sa'=2] {'af'}, use_global_device_ids=true, to_apply=%add.1 | all-reduce | flops 64 | bytes 512
  462.6 2.2 copy.163
  464.9 3.5 multiply_reduce_fusion.1
  470.3 2.7 reduce_sum.167
  473.0 2.3 fusion.43
  475.3 2.0 reduce_sum.166
  478.5 38.7 %all-reduce.2 = f32[64]{0:T(128)S(1)} all-reduce(f32[64]{0:T(128)S(1)} %dynamic-update-slice.2), channel_id=4, replica_groups=mesh['af'=16,'sa'=2] {'af'}, use_global_device_ids=true, to_apply=%add.2 | all-reduce | flops 64 | bytes 512
  517.4 2.2 copy.166
  519.7 3.5 multiply_reduce_fusion
  525.2 2.7 reduce_sum.171
  530.3 7.3 %fusion.2 = f32[4,10,16384]{2,1,0:T(8,128)S(1)} fusion(f32[4,10,16384]{2,0,1:T(4,128)S(1)} %reshape.266, f32[1,10,10]{2,0,1:T(1,128)S(1)} %get-tuple-element.23), kind=kOutput, calls=%fused_computation.4 | convolution fusion | flops 79298560 | bytes 5243280 | tf_op jit(solution)/shard_map/jk,skf->sjf/dot_general | solution.py:90
  537.7 9.1 %fusion.82 = f32[4,16384]{1,0:T(4,128)S(1)} fusion(f32[4,10,16384]{2,1,0:T(8,128)S(1)} %fusion.2, f32[4,10,16384]{2,0,1:T(4,128)S(1)} %copy-done, f32[1,10,10]{2,0,1:T(1,128)S(1)} %get-tuple-element.23), kind=kOutput, calls=%fused_computation.85 | convolution fusion | flops 80543744 | bytes 5505424 | tf_op jit(solution)/shard_map/jk,skf->sjf/dot_general | solution.py:91
  547.0 7.3 %fusion.5 = f32[4,10,16384]{2,1,0:T(8,128)S(1)} fusion(f32[4,10,16384]{2,0,1:T(4,128)S(1)} %reshape.266, f32[1,10,10]{2,0,1:T(1,128)S(1)} %get-tuple-element.21), kind=kOutput, calls=%fused_computation.9 | convolution fusion | flops 79298560 | bytes 5243280 | tf_op jit(solution)/shard_map/jk,skf->sjf/dot_general | solution.py:90
  554.3 8.9 %fusion.79 = f32[4,16384]{1,0:T(4,128)S(1)} fusion(f32[4,10,16384]{2,1,0:T(8,128)S(1)} %fusion.5, f32[4,10,16384]{2,0,1:T(4,128)S(1)} %copy-done, f32[1,10,10]{2,0,1:T(1,128)S(1)} %get-tuple-element.21), kind=kOutput, calls=%fused_computation.84 | convolution fusion | flops 80543744 | bytes 5505424 | tf_op jit(solution)/shard_map/jk,skf->sjf/dot_general | solution.py:91
  563.4 7.3 %fusion.8 = f32[4,10,16384]{2,1,0:T(8,128)S(1)} fusion(f32[4,10,16384]{2,0,1:T(4,128)S(1)} %reshape.266, f32[1,10,10]{2,0,1:T(1,128)S(1)} %get-tuple-element.22), kind=kOutput, calls=%fused_computation.14 | convolution fusion | flops 79298560 | bytes 5243280 | tf_op jit(solution)/shard_map/jk,skf->sjf/dot_general | solution.py:90
  570.8 8.9 %fusion.76 = f32[4,16384]{1,0:T(4,128)S(1)} fusion(f32[4,10,16384]{2,1,0:T(8,128)S(1)} %fusion.8, f32[4,10,16384]{2,0,1:T(4,128)S(1)} %copy-done, f32[1,10,10]{2,0,1:T(1,128)S(1)} %get-tuple-element.22), kind=kOutput, calls=%fused_computation.83 | convolution fusion | flops 80543744 | bytes 5505424 | tf_op jit(solution)/shard_map/jk,skf->sjf/dot_general | solution.py:91
  579.9 7.3 %fusion.11 = f32[4,10,16384]{2,1,0:T(8,128)S(1)} fusion(f32[4,10,16384]{2,0,1:T(4,128)S(1)} %reshape.266, f32[1,10,10]{2,0,1:T(1,128)S(1)} %get-tuple-element.20), kind=kOutput, calls=%fused_computation.19 | convolution fusion | flops 79298560 | bytes 5243280 | tf_op jit(solution)/shard_map/jk,skf->sjf/dot_general | solution.py:90
  587.2 9.0 %fusion.73 = f32[4,16384]{1,0:T(4,128)S(1)} fusion(f32[4,10,16384]{2,1,0:T(8,128)S(1)} %fusion.11, f32[4,10,16384]{2,0,1:T(4,128)S(1)} %copy-done, f32[1,10,10]{2,0,1:T(1,128)S(1)} %get-tuple-element.20), kind=kOutput, calls=%fused_computation.82 | convolution fusion | flops 80543744 | bytes 5505424 | tf_op jit(solution)/shard_map/jk,skf->sjf/dot_general | solution.py:91
  (72 shorter events, 28.1 us)
Async XLA Ops:
  2.3 18.2 %all-to-all-start.1 = ((f32[4,16,1024]{2,0,1:T(4,128)}), f32[4,16,1024]{2,0,1:T(4,128)S(1)}, u32[]{:S(2)}, u32[]{:S(2)}) async-start(f32[4,16,1024]{2,0,1:T(4,128)} %bitcast.5), calls=%async_computation.1 | async-start | bytes 524288 | tf_op jit(solution)/shard_map/all_to_all | solution.py:32
  20.6 27.3 %all-to-all-start = ((f32[10,16,1024]{2,0,1:T(8,128)}), f32[10,16,1024]{2,0,1:T(8,128)S(1)}, u32[]{:S(2)}, u32[]{:S(2)}) async-start(f32[10,16,1024]{2,0,1:T(8,128)} %copy.150), calls=%async_computation | async-start | bytes 2097152 | tf_op jit(solution)/shard_map/all_to_all | solution.py:39
  58.5 56.7 %all-to-all-start.3 = ((f32[4,10,16,1024]{3,0,1,2:T(4,128)}), f32[4,10,16,1024]{3,0,1,2:T(4,128)S(1)}, u32[]{:S(2)}, u32[]{:S(2)}) async-start(f32[4,10,16,1024]{3,0,1,2:T(4,128)} %copy.155), calls=%async_computation.3 | async-start | bytes 5242880 | tf_op jit(solution)/shard_map/all_to_all | solution.py:60
  69.3 58.2 %copy-start.9 = (u32[32]{0:T(128)S(1)}, u32[32]{0:T(128)}, u32[]{:S(2)}) copy-start(u32[32]{0:T(128)} %constant.83) | copy-start | bytes 388
  69.3 59.7 %copy-start.8 = (f32[10]{0:T(128)S(1)}, f32[10]{0:T(128)}, u32[]{:S(2)}) copy-start(f32[10]{0:T(128)} %param.6) | copy-start | bytes 124
  69.3 59.7 %copy-start.7 = (f32[4,10,10]{2,0,1:T(4,128)S(1)}, f32[4,10,10]{2,0,1:T(4,128)}, u32[]{:S(2)}) copy-start(f32[4,10,10]{2,0,1:T(4,128)} %param.7) | copy-start | bytes 4804
  115.2 63.6 %all-to-all-start.2 = ((f32[4,10,16,1024]{3,0,1,2:T(4,128)}), f32[4,10,16,1024]{3,0,1,2:T(4,128)}, u32[]{:S(2)}, u32[]{:S(2)}) async-start(f32[4,10,16,1024]{3,0,1,2:T(4,128)} %copy.153), calls=%async_computation.2 | async-start | bytes 5242880 | tf_op jit(solution)/shard_map/all_to_all | solution.py:59
  139.2 45.7 %copy-start.3 = (f32[16,4,10,1024]{3,0,2,1:T(8,128)S(1)}, f32[16,4,10,1024]{3,0,2,1:T(8,128)}, u32[]{:S(2)}) copy-start(f32[16,4,10,1024]{3,0,2,1:T(8,128)} %fusion.47) | copy-start | bytes 7864324
  184.9 67.5 %copy-start.4 = (f32[16,4,10,1024]{3,0,2,1:T(8,128)}, f32[16,4,10,1024]{3,0,2,1:T(8,128)S(1)}, u32[]{:S(2)}) copy-start(f32[16,4,10,1024]{3,0,2,1:T(8,128)S(1)} %fusion.70) | copy-start | bytes 7864324
  202.1 50.3 %copy-start.5 = (f32[16,4,10,1024]{3,0,2,1:T(8,128)}, f32[16,4,10,1024]{3,0,2,1:T(8,128)S(1)}, u32[]{:S(2)}) copy-start(f32[16,4,10,1024]{3,0,2,1:T(8,128)S(1)} %fusion.67) | copy-start | bytes 7864324
  277.1 10.2 %copy-start.1 = (f32[4,10,1024,16]{2,3,1,0:T(8,128)}, f32[4,10,1024,16]{2,3,1,0:T(8,128)S(1)}, u32[]{:S(2)}) copy-start(f32[4,10,1024,16]{2,3,1,0:T(8,128)S(1)} %subtract_bitcast_fusion) | copy-start | bytes 7864324
  331.1 1.5 copy-start.2
  523.2 4.7 copy-start.6
  530.3 7.4 %copy-start = (f32[4,10,16384]{2,0,1:T(4,128)S(1)}, f32[4,10,16384]{2,0,1:T(4,128)}, u32[]{:S(2)}) copy-start(f32[4,10,16384]{2,0,1:T(4,128)} %reshape.267) | copy-start | bytes 7864324
